TPU v7x, 128 devices: a whole 4x4x4 slice. The times are simulated.
128 devices in a mesh: dev: 128 (over z, x, y, core).
Axes of the slice: x: 4, y: 4, z: 4, core: 2. Of those that a mesh axis runs over, the one named last changes fastest.
Arguments:
- embeddings: bfloat16 [131072, 128], P('dev'), may hold values from -6 to 6
- ranks: int32 [131072], P('dev'), may hold values from 0 to 131071, as said below
- pair_weight: bfloat16 [256, 128], replicated, may hold values from -0.375 to 0.375
- pair_bias: float32 [128], replicated, may hold values from -3 to 3
- score_weight: bfloat16 [128], replicated, may hold values from -0.5 to 0.5
Outputs:
- scores: float32 [31, 131072], P(None, 'dev')
Inputs may be any that keep to these rules, and one draw needn't show every extreme that they name: ranks is a permutation of 0 .. 131071. Of the records of one device, at most 16 have ranks in any one range [o * 1024, (o + 1) * 1024); on every device some range holds exactly 16 of them, and every range holds exactly 16 of some device's records.
All inputs are finite; a program needn't handle non-finite values.
Results may differ from a plain program's by a relative error of at most 0.0045.
Values may be sent and summed in bfloat16 or wider, within the bound.
A program may use at most 64 MiB of HBM per device.

v0:
```python
import jax
import jax.numpy as jnp
from jax import lax
from jax.sharding import PartitionSpec as P

WIN = 32


def from_behind(value, axis, steps):
    count = lax.axis_size(axis)
    initial, last = (max(0, -steps), min(count, count - steps))
    return lax.ppermute(value, axis, [(source, source + steps) for source in range(initial, last)])


def body(embeddings, ranks, pair_weight, pair_bias, score_weight):
    rows_dev = embeddings.shape[0]
    width = embeddings.shape[1]
    devices = lax.axis_size("dev")
    my_index = lax.axis_index("dev")
    margin = WIN - 1
    capacity = 2 * rows_dev // devices
    by_rank = jnp.argsort(ranks)
    ranked = ranks[by_rank]
    owners = ranked // rows_dev
    owner_ids = jnp.arange(devices, dtype=jnp.int32)
    member = owners[:, None] == owner_ids[None, :]
    counts = jnp.sum(member.astype(jnp.int32), axis=0)
    starts = jnp.cumsum(counts) - counts
    dropped = rows_dev + margin
    places = jnp.arange(capacity, dtype=jnp.int32)
    slot_index = jnp.clip(starts[:, None] + places[None, :], 0, rows_dev - 1)
    is_live = places[None, :] < counts[:, None]
    source_rows = by_rank[slot_index]
    target = jnp.where(is_live, ranked[slot_index] - owner_ids[:, None] * rows_dev, dropped)
    outgoing = embeddings[source_rows.reshape(-1)]
    arrived, positions = (
        lax.all_to_all(outgoing, "dev", split_axis=0, concat_axis=0, tiled=True),
        lax.all_to_all(target.reshape(-1), "dev", split_axis=0, concat_axis=0, tiled=True),
    )
    extended = (
        jnp.zeros((rows_dev + margin, width), jnp.bfloat16).at[positions].set(arrived, mode="drop")
    )
    local_rows = extended[:rows_dev]
    following = from_behind(local_rows[:margin], "dev", -1)
    extended = jnp.concatenate([local_rows, following], axis=0)
    leading = extended[:rows_dev].astype(jnp.float32)
    weight_product = pair_weight[:width]
    weight_distance = pair_weight[width:]

    def score_offset(offset):
        partner = lax.dynamic_slice_in_dim(extended, offset, rows_dev, 0).astype(jnp.float32)
        product = (leading * partner).astype(jnp.bfloat16)
        distance = jnp.abs(leading - partner).astype(jnp.bfloat16)
        hidden = jnp.dot(product, weight_product, preferred_element_type=jnp.float32)
        hidden = (
            hidden
            + jnp.dot(distance, weight_distance, preferred_element_type=jnp.float32)
            + pair_bias
        )
        hidden = jax.nn.relu(hidden).astype(jnp.bfloat16)
        return jnp.dot(hidden, score_weight, preferred_element_type=jnp.float32)

    offsets = jnp.arange(1, WIN, dtype=jnp.int32)
    scores = lax.map(score_offset, offsets)
    global_pos = my_index * rows_dev + jnp.arange(rows_dev, dtype=jnp.int32)
    inside = global_pos[None, :] + offsets[:, None] < devices * rows_dev
    return jnp.where(inside, scores, jnp.zeros_like(scores))


def solution(mesh):
    placed = (P("dev", None), P("dev"), P(), P(), P())
    return jax.shard_map(
        body, mesh=mesh, in_specs=placed, out_specs=P(None, "dev"), check_vma=False
    )
```

profile of v0, /device:TPU:1, one launch (start us, length us, event | category | flops | bytes accessed | tf_op | source)
XLA Modules:
  0.0 184.8 jit_solution(15574150520137605697)
XLA Ops:
  0.0 0.7 copy-done.1
  0.7 4.4 %sort.17 = (s32[1024]{0:T(1024)}, s32[1024]{0:T(1024)S(1)}) sort(s32[1024]{0:T(1024)S(1)} %copy-done.1, s32[1024]{0:T(1024)S(1)} %iota.35), dimensions={0}, to_apply=%region_0.0 | sort | flops 10240 | bytes 16384 | tf_op jit(solution)/shard_map/jit(argsort)/sort | solution.py:22
  5.1 4.5 %gather_fusion = s32[1024]{0:T(1024)S(1)} fusion(s32[1024]{0:T(1024)S(1)} %copy-done.1, s32[1024]{0:T(1024)S(1)} %fusion.25), kind=kCustom, calls=%fused_computation | custom fusion | bytes 12288 | tf_op jit(solution)/shard_map/gather | solution.py:23
  10.5 8.6 %gather_fusion.1 = s32[2048]{0:T(1024)S(1)} fusion(s32[1024]{0:T(1024)S(1)} %gather_fusion, s32[2048]{0:T(1024)S(1)} %broadcast_clamp_fusion.1), kind=kCustom, calls=%fused_computation.1 | custom fusion | bytes 24576 | tf_op jit(solution)/shard_map/gather | solution.py:34
  19.1 0.7 subtract_select_fusion
  19.9 11.5 %all-to-all-start = ((s32[128,16,1]{1,2,0:T(1,128)}), s32[128,16,1]{1,2,0:T(1,128)S(1)}, u32[]{:S(2)}, u32[]{:S(2)}) async-start(s32[128,16,1]{1,2,0:T(1,128)} %bitcast.4), calls=%async_computation | async-start | bytes 131072 | tf_op jit(solution)/shard_map/all_to_all | solution.py:38
  31.4 8.6 %gather_fusion.2 = s32[2048]{0:T(1024)S(1)} fusion(s32[1024]{0:T(1024)S(1)} %get-tuple-element.53, s32[2048]{0:T(1024)S(1)} %broadcast_clamp_fusion.1), kind=kCustom, calls=%fused_computation.2 | custom fusion | bytes 24576 | tf_op jit(solution)/shard_map/gather | solution.py:33
  40.1 8.0 %gather_fusion.3 = bf16[2048,128]{1,0:T(8,128)(2,1)} fusion(bf16[1024,128]{1,0:T(8,128)(2,1)S(1)} %copy-done, s32[2048]{0:T(1024)S(1)} %broadcast_clamp_fusion), kind=kCustom, calls=%fused_computation.3 | custom fusion | bytes 1056768 | tf_op jit(solution)/shard_map/gather | solution.py:35
  48.0 9.8 %all-to-all-start.1 = ((bf16[128,16,128]{2,1,0:T(8,128)(2,1)}), bf16[128,16,128]{2,1,0:T(8,128)(2,1)S(1)}, u32[]{:S(2)}, u32[]{:S(2)}) async-start(bf16[128,16,128]{2,1,0:T(8,128)(2,1)} %bitcast.8), calls=%async_computation.1 | async-start | bytes 1048576 | tf_op jit(solution)/shard_map/all_to_all | solution.py:37
  58.3 0.8 reduce.4
  59.3 12.1 %all-to-all-done.1 = bf16[128,16,128]{2,1,0:T(8,128)(2,1)S(1)} async-done(((bf16[128,16,128]{2,1,0:T(8,128)(2,1)}), bf16[128,16,128]{2,1,0:T(8,128)(2,1)S(1)}, u32[]{:S(2)}, u32[]{:S(2)}) %all-to-all-start.1) | async-done | bytes 524320 | tf_op jit(solution)/shard_map/all_to_all | solution.py:37
  71.4 5.7 %scatter_custom_fusion = bf16[1055,128]{1,0:T(8,128)(2,1)S(1)} fusion(s32[2048]{0:T(1024)S(1)} %bitcast.32, bf16[2048,128]{1,0:T(8,128)(2,1)S(1)} %bitcast.30, bf16[]{:T(256)} %constant.27.clone.1), kind=kCustom, calls=%fused_computation.28 | custom fusion | bytes 270082 | tf_op jit(solution)/shard_map/scatter | solution.py:41
  77.1 2.9 %collective-permute-start = (bf16[31,128]{1,0:T(8,128)(2,1)S(1)}, bf16[31,128]{1,0:T(8,128)(2,1)S(1)}, u32[]{:S(2)}, u32[]{:S(2)}) collective-permute-start(bf16[31,128]{1,0:T(8,128)(2,1)S(1)} %slice.26), channel_id=1, source_target_pairs={{1,0},{2,1},{3,2},{4,3},{5,4},{6,5},{7,6},{8,7},{9,8},{10,9},{11,1... | collective-permute-start | bytes 23816 | tf_op jit(solution)/shard_map/ppermute | solution.py:12
  80.1 2.0 %collective-permute-done = bf16[31,128]{1,0:T(8,128)(2,1)S(1)} collective-permute-done((bf16[31,128]{1,0:T(8,128)(2,1)S(1)}, bf16[31,128]{1,0:T(8,128)(2,1)S(1)}, u32[]{:S(2)}, u32[]{:S(2)}) %collective-permute-start) | collective-permute-done | bytes 7968 | tf_op jit(solution)/shard_map/ppermute | solution.py:12
  82.1 0.6 copy-done.3
  82.8 101.3 %while.11 = (s32[]{:T(128)}, f32[31,1024]{1,0:T(8,128)S(1)}, s32[31]{0:T(128)S(1)}, bf16[1055,128]{1,0:T(8,128)(2,1)S(1)}, f32[1024,128]{1,0:T(8,128)S(1)}, /*in...) while((s32[]{:T(128)}, f32[31,1024]{1,0:T(8,128)S(1)}, ...), condition=%wide.region_5.6_spmd.clone, body=%wide.region_4.5_spmd.sunk.clone | while | flops 68812800 | bytes 2700439 | solution.py:64
  86.0 0.6 dynamic_slice.24
  89.3 0.6 dynamic_slice.24
  92.6 0.6 dynamic_slice.24
  95.8 0.6 dynamic_slice.24
  102.3 0.6 dynamic_slice.24
  108.9 0.6 dynamic_slice.24
  115.4 0.6 dynamic_slice.24
  184.1 0.7 fusion.23
  (151 shorter events, 37.7 us)
Async XLA Ops:
  0.0 40.1 %copy-start = (bf16[1024,128]{1,0:T(8,128)(2,1)S(1)}, bf16[1024,128]{1,0:T(8,128)(2,1)}, u32[]{:S(2)}) copy-start(bf16[1024,128]{1,0:T(8,128)(2,1)} %param.7) | copy-start | bytes 786436
  0.0 0.7 copy-start.1
  19.9 28.2 %all-to-all-start = ((s32[128,16,1]{1,2,0:T(1,128)}), s32[128,16,1]{1,2,0:T(1,128)S(1)}, u32[]{:S(2)}, u32[]{:S(2)}) async-start(s32[128,16,1]{1,2,0:T(1,128)} %bitcast.4), calls=%async_computation | async-start | bytes 131072 | tf_op jit(solution)/shard_map/all_to_all | solution.py:38
  31.4 8.6 %copy-start.2 = (bf16[256,128]{1,0:T(8,128)(2,1)S(1)}, bf16[256,128]{1,0:T(8,128)(2,1)}, u32[]{:S(2)}) copy-start(bf16[256,128]{1,0:T(8,128)(2,1)} %param.9) | copy-start | bytes 196612
  48.0 23.3 %all-to-all-start.1 = ((bf16[128,16,128]{2,1,0:T(8,128)(2,1)}), bf16[128,16,128]{2,1,0:T(8,128)(2,1)S(1)}, u32[]{:S(2)}, u32[]{:S(2)}) async-start(bf16[128,16,128]{2,1,0:T(8,128)(2,1)} %bitcast.8), calls=%async_computation.1 | async-start | bytes 1048576 | tf_op jit(solution)/shard_map/all_to_all | solution.py:37
  77.1 5.0 %collective-permute-start = (bf16[31,128]{1,0:T(8,128)(2,1)S(1)}, bf16[31,128]{1,0:T(8,128)(2,1)S(1)}, u32[]{:S(2)}, u32[]{:S(2)}) collective-permute-start(bf16[31,128]{1,0:T(8,128)(2,1)S(1)} %slice.26), channel_id=1, source_target_pairs={{1,0},{2,1},{3,2},{4,3},{5,4},{6,5},{7,6},{8,7},{9,8},{10,9},{11,1... | collective-permute-start | bytes 23816 | tf_op jit(solution)/shard_map/ppermute | solution.py:12
  82.1 0.7 copy-start.3
  82.1 0.7 copy-start.4
where the time goes:
time: 186 us; the launch traced here: 185 us
  loops' own time  61.1 us (33%)
  local copies, waits for them, and re-layouts  58.5 us (31%)
  starting transfers between devices  24.2 us (13%)
  matrix products  19.3 us (10%)
  waiting for transfers between devices  14.1 us (8%)
  other arithmetic  7.37 us (4%)
    another operation x1, loops' own time, body(): scores = lax.map(score_offset, offsets)  61.1 us
    dynamic_slice x31, local copies, waits for them, and re-layouts, body(): scores = lax.map(score_offset, offsets)  18.2 us
    dot_general x31, matrix products, score_offset(): return jnp.dot(hidden, score_weight, preferred_element_type=jnp.float32)  12.1 us
    all_to_all x1, waiting for transfers between devices, body(): lax.all_to_all(outgoing, 'dev', split_axis=0, concat_axis=0, tiled=True)  12.1 us
    all_to_all x1, starting transfers between devices, body(): lax.all_to_all(target.reshape(-1), 'dev', split_axis=0, concat_axis=0, ti...  11.5 us
    all_to_all x1, starting transfers between devices, body(): lax.all_to_all(outgoing, 'dev', split_axis=0, concat_axis=0, tiled=True)  9.76 us
    gather x2, local copies, waits for them, and re-layouts, body(): ranked[slot_index] - owner_ids[:, None] * rows_dev  8.66 us
    gather x1, local copies, waits for them, and re-layouts, body(): source_rows = by_rank[slot_index]  8.58 us
  transfers between devices with their start and end apart: 3, of which 2 were waited for; matrix products, arithmetic and copies ran while one was open for 10% of the time, Pallas kernels for 0%

commit v1 on v0

v1 whole, which is shorter than its diff:
```python
import functools

import jax
import jax.numpy as jnp
from jax import lax
from jax.experimental import pallas as pl
from jax.experimental.pallas import tpu as pltpu
from jax.sharding import PartitionSpec as P

MESH = pl.DeviceIdType.MESH
WIN = 32
ROWS = 1024
CAP = 16
NDEV = 128
UNITS = 16
STRIDE = ROWS // UNITS
GROUPS = 8
GROUP_DEVS = NDEV // GROUPS
GROUP_ROWS = GROUP_DEVS * CAP
CHUNK = 256
F32, BF16 = jnp.float32, jnp.bfloat16


def iota(shape, dim):
    return lax.broadcasted_iota(jnp.int32, shape, dim)


def one_hot(labels, rows):
    lanes = jnp.broadcast_to(labels, (rows, 128)).astype(BF16)
    numbers = iota((rows, 128), 0).astype(F32).astype(BF16)
    return jnp.where(numbers == lanes, jnp.ones((), BF16), jnp.zeros((), BF16))


def within(values, low, size):
    moved = values - low
    return jnp.where((moved >= 0) & (moved < size), moved, -1.0)


def kernel(
    ranks_ref, emb_ref, weight_ref, bias_ref, score_ref, out_ref,
    send_rows, recv_rows, send_pos, recv_pos, acc, tiles, shifted, halo_out, halo_in, score_mats, packed,
    send_sem, pos_send_sem, pos_recv_sem, halo_send_sem, halo_recv_sem, recv_sems,
):
    me = lax.axis_index("dev")
    my_z, my_x, my_y, my_c = me // 32, (me // 8) % 4, (me // 2) % 4, me % 2

    barrier = pltpu.get_barrier_semaphore()

    def greet(base, carry):
        for j in range(8):
            pl.semaphore_signal(barrier, inc=1, device_id=(base * 8 + j,), device_id_type=MESH)
        return carry

    lax.fori_loop(0, NDEV // 8, greet, 0)

    ranks = ranks_ref[...]
    owner = ranks // ROWS
    local = ranks - owner * ROWS
    rel = (
        ((owner // 32 - my_z) & 3) * 32
        + (((owner // 8) - my_x) & 3) * 8
        + (((owner // 2) - my_y) & 3) * 2
        + ((owner - my_c) & 1)
    )
    place = (local % STRIDE) * UNITS + local // STRIDE + 1
    rel_f = rel.astype(F32)
    place_high = (place // 32).astype(F32)
    place_low = (place % 32).astype(F32)
    members = [one_hot(rel_f[a : a + 1], NDEV) for a in range(8)]
    prefix = jnp.where(
        (iota((128, 256), 0) <= iota((128, 256), 1)), jnp.ones((), F32), jnp.zeros((), F32)
    ).astype(BF16)
    counts = jnp.dot(jnp.concatenate(members, axis=0), prefix, preferred_element_type=F32)
    base = jnp.zeros((128, 128), F32)
    slots = []
    for a in range(8):
        block = counts[a * 128 : (a + 1) * 128]
        mine = members[a].astype(F32) * (block[:, :128] + base)
        slots.append(jnp.sum(mine, axis=0, keepdims=True) - 1.0)
        base = base + block[:, 128:]
    slot = jnp.concatenate(slots, axis=0)

    lane_slot = (iota((128, 128), 0) % CAP).astype(F32).astype(BF16)
    tables = []
    for a in range(8):
        here = jnp.broadcast_to(slot[a : a + 1], (128, 128)).astype(BF16) == lane_slot
        zero = jnp.zeros((128, 128), BF16)
        tables.append(
            jnp.concatenate(
                [
                    jnp.where(here, jnp.broadcast_to(place_high[a : a + 1], (128, 128)).astype(BF16), zero),
                    jnp.where(here, jnp.broadcast_to(place_low[a : a + 1], (128, 128)).astype(BF16), zero),
                ],
                axis=0,
            )
        )
    digits = lax.dot_general(
        jnp.concatenate(members, axis=1),
        jnp.concatenate(tables, axis=1),
        (((1,), (1,)), ((), ())),
        preferred_element_type=F32,
    )
    send_pos[...] = digits[:, :128] * 32.0 + digits[:, 128:]

    target = rel_f * CAP + slot

    def pack(group, carry):
        labels = within(target, (group * GROUP_ROWS).astype(F32), GROUP_ROWS)
        choose = jnp.concatenate([one_hot(labels[a : a + 1], GROUP_ROWS) for a in range(8)], axis=1)
        rows = jnp.dot(choose, emb_ref[...], preferred_element_type=F32).astype(BF16)
        send_rows[pl.ds(pl.multiple_of(group * GROUP_ROWS, GROUP_ROWS), GROUP_ROWS), :] = rows
        return carry

    lax.fori_loop(0, GROUPS, pack, 0)

    columns = [((my_y + dy) % 4) * 2 + (my_c + dc) % 2 for dy in range(4) for dc in range(2)]

    def plane(step):
        return (((my_z + step // 4) % 4) * 4 + (my_x + step % 4) % 4) * 8

    def row_copy(step, j, base_id):
        part = pl.ds(pl.multiple_of((step * 8 + j) * CAP, CAP), CAP)
        return pltpu.make_async_remote_copy(
            src_ref=send_rows.at[part], dst_ref=recv_rows.at[part],
            send_sem=send_sem, recv_sem=recv_sems.at[step // 2],
            device_id=(base_id + columns[j],), device_id_type=MESH,
        )

    def pos_copy(step, j, base_id):
        part = pl.ds(step * 8 + j, 1)
        return pltpu.make_async_remote_copy(
            src_ref=send_pos.at[part], dst_ref=recv_pos.at[part],
            send_sem=pos_send_sem, recv_sem=pos_recv_sem,
            device_id=(base_id + columns[j],), device_id_type=MESH,
        )

    pl.semaphore_wait(barrier, NDEV)
    here = plane(0)
    for j in range(1, 8):
        pos_copy(0, j, here).start()
        row_copy(0, j, here).start()

    def send(step, carry):
        base_id = plane(step)
        for j in range(8):
            pos_copy(step, j, base_id).start()
            row_copy(step, j, base_id).start()
        return carry

    lax.fori_loop(1, 16, send, 0)

    recv_rows[:CAP, :] = send_rows[:CAP, :]
    recv_pos[0:1, :] = send_pos[0:1, :]

    column = jnp.transpose(jnp.broadcast_to(score_ref[...].astype(F32), (128, 128)))
    lane = iota((128, 128), 1)
    for k in range(WIN - 1):
        score_mats[k * 128 : (k + 1) * 128, :] = jnp.where(lane == k, column, 0.0).astype(BF16)

    rest = pl.ds(1, NDEV - 1)
    whole = pltpu.make_async_remote_copy(
        src_ref=send_pos.at[rest], dst_ref=recv_pos.at[rest], send_sem=pos_send_sem, recv_sem=pos_recv_sem,
        device_id=(me,), device_id_type=MESH,
    )
    whole.wait_send()
    whole.wait_recv()
    keep = (iota((NDEV, 128), 0) % 8) == (iota((NDEV, 128), 1) // CAP)
    wanted = jnp.sum(jnp.where(keep, recv_pos[...], 0.0).reshape(16, 8, 128), axis=1) - 1.0

    for group in range(GROUPS):
        first = CAP if group == 0 else group * GROUP_ROWS
        part = pl.ds(first, (group + 1) * GROUP_ROWS - first)
        pltpu.make_async_remote_copy(
            src_ref=send_rows.at[part], dst_ref=recv_rows.at[part],
            send_sem=send_sem, recv_sem=recv_sems.at[group], device_id=(me,), device_id_type=MESH,
        ).wait_recv()
        got = recv_rows[group * GROUP_ROWS : (group + 1) * GROUP_ROWS, :]
        for block in range(ROWS // CHUNK):
            labels = within(wanted[2 * group : 2 * group + 2], float(block * CHUNK), CHUNK)
            choose = jnp.concatenate([one_hot(labels[i : i + 1], CHUNK) for i in range(2)], axis=1)
            rows = jnp.dot(choose, got, preferred_element_type=F32)
            where = slice(block * CHUNK, (block + 1) * CHUNK)
            if group == 0:
                acc[where, :] = rows
            else:
                acc[where, :] = acc[where, :] + rows

    tiles[:ROWS, :] = acc[:ROWS, :].astype(BF16)

    halo_out[...] = acc[pl.ds(0, WIN, stride=UNITS), :].astype(BF16)
    before = lax.rem(me + NDEV - 1, NDEV)
    halo = pltpu.make_async_remote_copy(
        src_ref=halo_out, dst_ref=halo_in, send_sem=halo_send_sem, recv_sem=halo_recv_sem,
        device_id=(before,), device_id_type=MESH,
    )

    weight = weight_ref[...]
    bias = bias_ref[...]

    def score(chunk, carry):
        start = pl.multiple_of(chunk * CHUNK, CHUNK)
        leading = tiles[pl.ds(start, CHUNK), :]
        total = None
        for pair in range(WIN // 2):
            hiddens = []
            for k in (2 * pair + 1, 2 * pair + 2):
                if k == WIN:
                    continue
                partner = tiles[pl.ds(start + k * UNITS, CHUNK), :]
                features = jnp.concatenate([leading * partner, jnp.abs(leading - partner)], axis=1)
                hidden = jnp.dot(features, weight, preferred_element_type=F32) + bias
                hiddens.append(jnp.maximum(hidden.astype(BF16), jnp.zeros((), BF16)))
            hidden = jnp.concatenate(hiddens, axis=1) if len(hiddens) == 2 else hiddens[0]
            mats = score_mats[pair * 256 : pair * 256 + 128 * len(hiddens), :]
            term = jnp.dot(hidden, mats, preferred_element_type=F32)
            total = term if total is None else total + term
        packed[pl.ds(start, CHUNK), :] = total
        return carry

    halo.start()
    lax.fori_loop(0, 2, score, 0)
    halo.wait_send()
    halo.wait_recv()
    extra = (WIN - 1) * UNITS
    shifted[...] = acc[1 : 1 + extra + UNITS, :]
    shifted[pl.ds(UNITS - 1, WIN, stride=UNITS), :] = halo_in[...].astype(F32)
    tiles[ROWS : ROWS + extra, :] = shifted[:extra, :].astype(BF16)
    lax.fori_loop(2, 4, score, 0)

    offset = iota((WIN, 128), 0) + 1
    position = me * ROWS + iota((WIN, 128), 1)
    for block in range(8):
        rows = [packed[pl.ds(2 * block + i, STRIDE, stride=UNITS), :] for i in range(2)]
        turned = jnp.transpose(jnp.concatenate(rows, axis=0))[:WIN]
        inside = position + block * 128 + offset < NDEV * ROWS
        out_ref[:, block * 128 : (block + 1) * 128] = jnp.where(inside, turned, 0.0)[: WIN - 1]

    part = pl.ds(CAP, (NDEV - 1) * CAP)
    pltpu.make_async_remote_copy(
        src_ref=send_rows.at[part], dst_ref=recv_rows.at[part],
        send_sem=send_sem, recv_sem=recv_sems.at[0], device_id=(me,), device_id_type=MESH,
    ).wait_send()


def body(embeddings, ranks, pair_weight, pair_bias, score_weight):
    vmem = pl.BlockSpec(memory_space=pltpu.VMEM)
    return pl.pallas_call(
        kernel,
        out_shape=jax.ShapeDtypeStruct((WIN - 1, ROWS), F32),
        in_specs=[vmem] * 5,
        out_specs=vmem,
        scratch_shapes=[
            pltpu.VMEM((NDEV * CAP, 128), BF16),
            pltpu.VMEM((NDEV * CAP, 128), BF16),
            pltpu.VMEM((NDEV, 128), F32),
            pltpu.VMEM((NDEV, 128), F32),
            pltpu.VMEM((ROWS + 8, 128), F32),
            pltpu.VMEM((ROWS + WIN * UNITS, 128), BF16),
            pltpu.VMEM((WIN * UNITS, 128), F32),
            pltpu.VMEM((WIN, 128), BF16),
            pltpu.VMEM((WIN, 128), BF16),
            pltpu.VMEM((WIN * 128, 128), BF16),
            pltpu.VMEM((ROWS, 128), F32),
            pltpu.SemaphoreType.DMA,
            pltpu.SemaphoreType.DMA,
            pltpu.SemaphoreType.DMA,
            pltpu.SemaphoreType.DMA,
            pltpu.SemaphoreType.DMA,
            pltpu.SemaphoreType.DMA((GROUPS,)),
        ],
        compiler_params=pltpu.CompilerParams(collective_id=0, has_side_effects=True),
        name="neighborhood_scores",
    )(
        ranks.reshape(8, 128),
        embeddings,
        pair_weight,
        pair_bias.reshape(1, 128),
        score_weight.reshape(1, 128),
    )


def solution(mesh):
    placed = (P("dev", None), P("dev"), P(), P(), P())
    return jax.shard_map(
        body, mesh=mesh, in_specs=placed, out_specs=P(None, "dev"), check_vma=False
    )
```

time: 186 us -> 39.9 us (0.21)
  loops' own time: 61.1 us -> 0 us
  local copies, waits for them, and re-layouts: 58.5 us -> 1.57 us
  Pallas kernels: 0 us -> 38.2 us
  starting transfers between devices: 24.2 us -> 0 us
  matrix products: 19.3 us -> 0 us
  waiting for transfers between devices: 14.1 us -> 0 us
  other arithmetic: 7.37 us -> 0 us
    another operation x1 -> x0, loops' own time: 61.1 us -> none  [body(): scores = lax.map(score_offset, offsets)]
    pallas_call x0 -> x1, Pallas kernels: none -> 38.2 us  [body(): pl.pallas_call(kernel, out_shape=jax.ShapeDtypeStruct((WIN - 1, ROWS), F3...]
    gather x5 -> x0, local copies, waits for them, and re-layouts: 29.7 us -> none  [the longest x2 8.66 us: body(): ranked[slot_index] - owner_ids[:, None] * rows_dev]
    all_to_all x2 -> x0, starting transfers between devices: 21.2 us -> none  [the longest x1 11.5 us: body(): lax.all_to_all(target.reshape(-1), 'dev', split_axis=0, concat_axis=0, ti...]
    dot_general x62 -> x0, matrix products: 19.3 us -> none  [the longest x31 12.1 us: score_offset(): return jnp.dot(hidden, score_weight, preferred_element_type=jnp.float32)]
    dynamic_slice x31 -> x0, local copies, waits for them, and re-layouts: 18.2 us -> none  [body(): scores = lax.map(score_offset, offsets)]
    all_to_all x2 -> x0, waiting for transfers between devices: 12.1 us -> none  [the longest x1 12.1 us: body(): lax.all_to_all(outgoing, 'dev', split_axis=0, concat_axis=0, tiled=True)]
    scatter x1 -> x0, local copies, waits for them, and re-layouts: 5.74 us -> none  [body(): jnp.zeros((rows_dev + margin, width), jnp.bfloat16).at[positions]]
  transfers between devices with their start and end apart: 3 -> 0, of which waited for: 2 -> 0; matrix products, arithmetic and copies ran while one was open for 10% -> 0% of each run, Pallas kernels for 0% -> 0%
where the time goes in v1:
time: 39.9 us; the launch traced here: 39.8 us
  Pallas kernels  38.2 us (96%)
  local copies, waits for them, and re-layouts  1.57 us (4%)
    pallas_call x1, Pallas kernels, body(): pl.pallas_call(kernel, out_shape=jax.ShapeDtypeStruct((WIN - 1, ROWS), F3...  38.2 us
    unnamed x1, local copies, waits for them, and re-layouts  1.57 us

profile of v1, /device:TPU:1, one launch (start us, length us, event | category | flops | bytes accessed | tf_op | source)
XLA Modules:
  0.0 39.8 jit_solution(17927300091851559905)
XLA Ops:
  0.0 38.2 %neighborhood_scores.1 = f32[31,1024]{1,0:T(8,128)} custom-call(s32[8,128]{1,0:T(8,128)} %bitcast.3, bf16[1024,128]{1,0:T(8,128)(2,1)} %emb_ref.1, bf16[256,128]{1,0:T(8,128)(2,1)} %weight_ref.1, f32[1,128]{1,0:T(1,128)} %bitcast.4, bf16[1,128]{1,0:T(2,128)(2,1)} %bitcast.5), custom_call_target="tpu_custom_call" | custom-call | tf_op jit(solution)/shard_map/neighborhood_scores/pallas_call | solution.py:247
  38.2 1.6 %copy.7 = f32[31,1024]{1,0:T(8,128)} copy(f32[31,1024]{1,0:T(8,128)} %neighborhood_scores.1) | data formatting | bytes 253952

commit v2 on v1

--- a/solution.py
+++ b/solution.py
@@ -17,7 +17,8 @@
 GROUPS = 8
 GROUP_DEVS = NDEV // GROUPS
 GROUP_ROWS = GROUP_DEVS * CAP
-CHUNK = 256
+CHUNK = 512
+PLACES = 256
 F32, BF16 = jnp.float32, jnp.bfloat16
 
 
@@ -37,13 +38,17 @@
 
 
 def kernel(
-    ranks_ref, emb_ref, weight_ref, bias_ref, score_ref, out_ref,
-    send_rows, recv_rows, send_pos, recv_pos, acc, tiles, shifted, halo_out, halo_in, score_mats, packed,
-    send_sem, pos_send_sem, pos_recv_sem, halo_send_sem, halo_recv_sem, recv_sems,
+    ranks_ref, emb_hbm, weight_hbm, bias_ref, score_ref, out_ref,
+    emb_ref, weight_ref, send_rows, recv_rows, send_pos, recv_pos, tiles, halo_out, halo_in, packed,
+    load_sems, send_sem, pos_send_sem, pos_recv_sem, halo_send_sem, halo_recv_sem, recv_sems,
 ):
     me = lax.axis_index("dev")
     my_z, my_x, my_y, my_c = me // 32, (me // 8) % 4, (me // 2) % 4, me % 2
 
+    load_emb = pltpu.make_async_copy(emb_hbm, emb_ref, load_sems.at[0])
+    load_weight = pltpu.make_async_copy(weight_hbm, weight_ref, load_sems.at[1])
+    load_emb.start()
+    load_weight.start()
     barrier = pltpu.get_barrier_semaphore()
 
     def greet(base, carry):
@@ -104,14 +109,13 @@
 
     target = rel_f * CAP + slot
 
-    def pack(group, carry):
-        labels = within(target, (group * GROUP_ROWS).astype(F32), GROUP_ROWS)
+    load_emb.wait()
+    emb = emb_ref[...]
+    for group in range(GROUPS):
+        labels = within(target, float(group * GROUP_ROWS), GROUP_ROWS)
         choose = jnp.concatenate([one_hot(labels[a : a + 1], GROUP_ROWS) for a in range(8)], axis=1)
-        rows = jnp.dot(choose, emb_ref[...], preferred_element_type=F32).astype(BF16)
-        send_rows[pl.ds(pl.multiple_of(group * GROUP_ROWS, GROUP_ROWS), GROUP_ROWS), :] = rows
-        return carry
-
-    lax.fori_loop(0, GROUPS, pack, 0)
+        rows = jnp.dot(choose, emb, preferred_element_type=F32).astype(BF16)
+        send_rows[group * GROUP_ROWS : (group + 1) * GROUP_ROWS, :] = rows
 
     columns = [((my_y + dy) % 4) * 2 + (my_c + dc) % 2 for dy in range(4) for dc in range(2)]
 
@@ -151,11 +155,6 @@
 
     recv_rows[:CAP, :] = send_rows[:CAP, :]
     recv_pos[0:1, :] = send_pos[0:1, :]
-
-    column = jnp.transpose(jnp.broadcast_to(score_ref[...].astype(F32), (128, 128)))
-    lane = iota((128, 128), 1)
-    for k in range(WIN - 1):
-        score_mats[k * 128 : (k + 1) * 128, :] = jnp.where(lane == k, column, 0.0).astype(BF16)
 
     rest = pl.ds(1, NDEV - 1)
     whole = pltpu.make_async_remote_copy(
@@ -175,57 +174,45 @@
             send_sem=send_sem, recv_sem=recv_sems.at[group], device_id=(me,), device_id_type=MESH,
         ).wait_recv()
         got = recv_rows[group * GROUP_ROWS : (group + 1) * GROUP_ROWS, :]
-        for block in range(ROWS // CHUNK):
-            labels = within(wanted[2 * group : 2 * group + 2], float(block * CHUNK), CHUNK)
-            choose = jnp.concatenate([one_hot(labels[i : i + 1], CHUNK) for i in range(2)], axis=1)
+        for block in range(ROWS // PLACES):
+            labels = within(wanted[2 * group : 2 * group + 2], float(block * PLACES), PLACES)
+            choose = jnp.concatenate([one_hot(labels[i : i + 1], PLACES) for i in range(2)], axis=1)
             rows = jnp.dot(choose, got, preferred_element_type=F32)
-            where = slice(block * CHUNK, (block + 1) * CHUNK)
+            where = slice(block * PLACES, (block + 1) * PLACES)
             if group == 0:
-                acc[where, :] = rows
+                tiles[where, :] = rows
             else:
-                acc[where, :] = acc[where, :] + rows
-
-    tiles[:ROWS, :] = acc[:ROWS, :].astype(BF16)
-
-    halo_out[...] = acc[pl.ds(0, WIN, stride=UNITS), :].astype(BF16)
+                tiles[where, :] = tiles[where, :] + rows
+
+    halo_out[...] = tiles[pl.ds(0, WIN, stride=UNITS), :].astype(BF16)
     before = lax.rem(me + NDEV - 1, NDEV)
     halo = pltpu.make_async_remote_copy(
         src_ref=halo_out, dst_ref=halo_in, send_sem=halo_send_sem, recv_sem=halo_recv_sem,
         device_id=(before,), device_id_type=MESH,
     )
 
+    load_weight.wait()
     weight = weight_ref[...]
     bias = bias_ref[...]
-
-    def score(chunk, carry):
-        start = pl.multiple_of(chunk * CHUNK, CHUNK)
-        leading = tiles[pl.ds(start, CHUNK), :]
-        total = None
-        for pair in range(WIN // 2):
-            hiddens = []
-            for k in (2 * pair + 1, 2 * pair + 2):
-                if k == WIN:
-                    continue
-                partner = tiles[pl.ds(start + k * UNITS, CHUNK), :]
-                features = jnp.concatenate([leading * partner, jnp.abs(leading - partner)], axis=1)
-                hidden = jnp.dot(features, weight, preferred_element_type=F32) + bias
-                hiddens.append(jnp.maximum(hidden.astype(BF16), jnp.zeros((), BF16)))
-            hidden = jnp.concatenate(hiddens, axis=1) if len(hiddens) == 2 else hiddens[0]
-            mats = score_mats[pair * 256 : pair * 256 + 128 * len(hiddens), :]
-            term = jnp.dot(hidden, mats, preferred_element_type=F32)
-            total = term if total is None else total + term
-        packed[pl.ds(start, CHUNK), :] = total
-        return carry
+    score_weight = score_ref[...].astype(F32)
+
+    def score(start):
+        leading = tiles[start : start + CHUNK, :].astype(BF16)
+        for k in range(1, WIN):
+            partner = tiles[start + k * UNITS : start + k * UNITS + CHUNK, :].astype(BF16)
+            features = jnp.concatenate([leading * partner, jnp.abs(leading - partner)], axis=1)
+            hidden = jnp.dot(features, weight, preferred_element_type=F32) + bias
+            hidden = jnp.maximum(hidden, 0.0)
+            packed[start : start + CHUNK, k - 1 : k] = jnp.sum(hidden * score_weight, axis=1, keepdims=True)
 
     halo.start()
-    lax.fori_loop(0, 2, score, 0)
+    score(0)
     halo.wait_send()
     halo.wait_recv()
     extra = (WIN - 1) * UNITS
-    shifted[...] = acc[1 : 1 + extra + UNITS, :]
-    shifted[pl.ds(UNITS - 1, WIN, stride=UNITS), :] = halo_in[...].astype(F32)
-    tiles[ROWS : ROWS + extra, :] = shifted[:extra, :].astype(BF16)
-    lax.fori_loop(2, 4, score, 0)
+    tiles[ROWS : ROWS + extra, :] = tiles[1 : 1 + extra, :]
+    tiles[pl.ds(ROWS + UNITS - 1, WIN, stride=UNITS), :] = halo_in[...].astype(F32)
+    score(CHUNK)
 
     offset = iota((WIN, 128), 0) + 1
     position = me * ROWS + iota((WIN, 128), 1)
@@ -244,23 +231,24 @@
 
 def body(embeddings, ranks, pair_weight, pair_bias, score_weight):
     vmem = pl.BlockSpec(memory_space=pltpu.VMEM)
+    hbm = pl.BlockSpec(memory_space=pl.ANY)
     return pl.pallas_call(
         kernel,
         out_shape=jax.ShapeDtypeStruct((WIN - 1, ROWS), F32),
-        in_specs=[vmem] * 5,
+        in_specs=[vmem, hbm, hbm, vmem, vmem],
         out_specs=vmem,
         scratch_shapes=[
+            pltpu.VMEM((ROWS, 128), BF16),
+            pltpu.VMEM((256, 128), BF16),
             pltpu.VMEM((NDEV * CAP, 128), BF16),
             pltpu.VMEM((NDEV * CAP, 128), BF16),
             pltpu.VMEM((NDEV, 128), F32),
             pltpu.VMEM((NDEV, 128), F32),
-            pltpu.VMEM((ROWS + 8, 128), F32),
-            pltpu.VMEM((ROWS + WIN * UNITS, 128), BF16),
-            pltpu.VMEM((WIN * UNITS, 128), F32),
+            pltpu.VMEM((ROWS + WIN * UNITS, 128), F32),
             pltpu.VMEM((WIN, 128), BF16),
             pltpu.VMEM((WIN, 128), BF16),
-            pltpu.VMEM((WIN * 128, 128), BF16),
             pltpu.VMEM((ROWS, 128), F32),
+            pltpu.SemaphoreType.DMA((2,)),
             pltpu.SemaphoreType.DMA,
             pltpu.SemaphoreType.DMA,
             pltpu.SemaphoreType.DMA,

time: 39.9 us -> 31.3 us (0.78)
  Pallas kernels: 38.2 us -> 29.6 us
    pallas_call x1, Pallas kernels: 38.2 us -> 29.6 us  [body(): pl.pallas_call(kernel, out_shape=jax.ShapeDtypeStruct((WIN - 1, ROWS), F3...]
where the time goes in v2:
time: 31.3 us; the launch traced here: 31.2 us
  Pallas kernels  29.6 us (95%)
  local copies, waits for them, and re-layouts  1.57 us (5%)
    pallas_call x1, Pallas kernels, body(): pl.pallas_call(kernel, out_shape=jax.ShapeDtypeStruct((WIN - 1, ROWS), F3...  29.6 us
    unnamed x1, local copies, waits for them, and re-layouts  1.57 us

profile of v2, /device:TPU:1, one launch (start us, length us, event | category | flops | bytes accessed | tf_op | source)
XLA Modules:
  0.0 31.2 jit_solution(7065052034996725079)
XLA Ops:
  0.0 29.6 %neighborhood_scores.1 = f32[31,1024]{1,0:T(8,128)} custom-call(s32[8,128]{1,0:T(8,128)} %bitcast.3, bf16[1024,128]{1,0:T(8,128)(2,1)} %emb_hbm.1, bf16[256,128]{1,0:T(8,128)(2,1)} %weight_hbm.1, f32[1,128]{1,0:T(1,128)} %bitcast.4, bf16[1,128]{1,0:T(2,128)(2,1)} %bitcast.5), custom_call_target="tpu_custom_call" | custom-call | tf_op jit(solution)/shard_map/neighborhood_scores/pallas_call | solution.py:235
  29.6 1.6 %copy.7 = f32[31,1024]{1,0:T(8,128)} copy(f32[31,1024]{1,0:T(8,128)} %neighborhood_scores.1) | data formatting | bytes 253952

commit v3 on v2

--- a/solution.py
+++ b/solution.py
@@ -19,6 +19,7 @@
 GROUP_ROWS = GROUP_DEVS * CAP
 CHUNK = 512
 PLACES = 256
+SPLIT = 7
 F32, BF16 = jnp.float32, jnp.bfloat16
 
 
@@ -38,35 +39,47 @@
 
 
 def kernel(
-    ranks_ref, emb_hbm, weight_hbm, bias_ref, score_ref, out_ref,
-    emb_ref, weight_ref, send_rows, recv_rows, send_pos, recv_pos, tiles, halo_out, halo_in, packed,
-    load_sems, send_sem, pos_send_sem, pos_recv_sem, halo_send_sem, halo_recv_sem, recv_sems,
+    ranks_hbm, emb_hbm, weight_hbm, bias_hbm, score_hbm, out_ref,
+    ranks_ref, emb_ref, weight_ref, bias_ref, score_ref,
+    send_rows, recv_rows, send_pos, plane_pos, recv_pos, tiles, halo_out, halo_in, packed,
+    load_sems, ready_sem, send_sem, plane_send_sem, plane_recv_sem, pos_send_sem, pos_recv_sem,
+    halo_send_sem, halo_recv_sem, recv_sems,
 ):
     me = lax.axis_index("dev")
     my_z, my_x, my_y, my_c = me // 32, (me // 8) % 4, (me // 2) % 4, me % 2
 
-    load_emb = pltpu.make_async_copy(emb_hbm, emb_ref, load_sems.at[0])
-    load_weight = pltpu.make_async_copy(weight_hbm, weight_ref, load_sems.at[1])
-    load_emb.start()
-    load_weight.start()
+    loads = [
+        pltpu.make_async_copy(source, target, load_sems.at[i])
+        for i, (source, target) in enumerate(
+            [
+                (ranks_hbm, ranks_ref), (emb_hbm, emb_ref), (weight_hbm, weight_ref),
+                (bias_hbm, bias_ref), (score_hbm, score_ref),
+            ]
+        )
+    ]
+    for load in loads:
+        load.start()
+
+    columns = [((my_y + dy) % 4) * 2 + (my_c + dc) % 2 for dy in range(4) for dc in range(2)]
+
+    def plane(step):
+        step = (step * 5) % 16
+        return (((my_z + step // 4) % 4) * 4 + (my_x + step % 4) % 4) * 8
+
     barrier = pltpu.get_barrier_semaphore()
-
-    def greet(base, carry):
-        for j in range(8):
-            pl.semaphore_signal(barrier, inc=1, device_id=(base * 8 + j,), device_id_type=MESH)
-        return carry
-
-    lax.fori_loop(0, NDEV // 8, greet, 0)
-
+    planes = [plane(step) for step in range(16)]
+    plane_mates = [planes[step] + columns[0] for step in range(1, 16)]
+    column_mates = [planes[0] + columns[j] for j in range(1, 8)]
+    for mate in plane_mates + column_mates:
+        pl.semaphore_signal(barrier, inc=1, device_id=(mate,), device_id_type=MESH)
+
+    loads[0].wait()
     ranks = ranks_ref[...]
     owner = ranks // ROWS
     local = ranks - owner * ROWS
-    rel = (
-        ((owner // 32 - my_z) & 3) * 32
-        + (((owner // 8) - my_x) & 3) * 8
-        + (((owner // 2) - my_y) & 3) * 2
-        + ((owner - my_c) & 1)
-    )
+    plane_rel = ((owner // 32 - my_z) & 3) * 4 + ((owner // 8 - my_x) & 3)
+    column_rel = ((owner // 2 - my_y) & 3) * 2 + ((owner - my_c) & 1)
+    rel = ((plane_rel * 13) & 15) * 8 + column_rel
     place = (local % STRIDE) * UNITS + local // STRIDE + 1
     rel_f = rel.astype(F32)
     place_high = (place // 32).astype(F32)
@@ -105,22 +118,31 @@
         (((1,), (1,)), ((), ())),
         preferred_element_type=F32,
     )
-    send_pos[...] = digits[:, :128] * 32.0 + digits[:, 128:]
+    places = digits[:, :128] * 32.0 + digits[:, 128:]
+    keep = (iota((NDEV, 128), 0) % 8) == (iota((NDEV, 128), 1) // CAP)
+    by_step = jnp.sum(jnp.where(keep, places, 0.0).reshape(16, 8, 128), axis=1)
+    send_pos[...] = by_step
+    plane_pos[0:1, :] = by_step[0:1]
+
+    pl.semaphore_wait(barrier, 22)
+    for mate in column_mates:
+        pl.semaphore_signal(ready_sem, inc=1, device_id=(mate,), device_id_type=MESH)
+    for step in range(1, 16):
+        pltpu.make_async_remote_copy(
+            src_ref=send_pos.at[pl.ds(step, 1)], dst_ref=plane_pos.at[pl.ds(step, 1)],
+            send_sem=plane_send_sem, recv_sem=plane_recv_sem,
+            device_id=(plane_mates[step - 1],), device_id_type=MESH,
+        ).start()
 
     target = rel_f * CAP + slot
 
-    load_emb.wait()
+    loads[1].wait()
     emb = emb_ref[...]
     for group in range(GROUPS):
         labels = within(target, float(group * GROUP_ROWS), GROUP_ROWS)
         choose = jnp.concatenate([one_hot(labels[a : a + 1], GROUP_ROWS) for a in range(8)], axis=1)
         rows = jnp.dot(choose, emb, preferred_element_type=F32).astype(BF16)
         send_rows[group * GROUP_ROWS : (group + 1) * GROUP_ROWS, :] = rows
-
-    columns = [((my_y + dy) % 4) * 2 + (my_c + dc) % 2 for dy in range(4) for dc in range(2)]
-
-    def plane(step):
-        return (((my_z + step // 4) % 4) * 4 + (my_x + step % 4) % 4) * 8
 
     def row_copy(step, j, base_id):
         part = pl.ds(pl.multiple_of((step * 8 + j) * CAP, CAP), CAP)
@@ -130,41 +152,46 @@
             device_id=(base_id + columns[j],), device_id_type=MESH,
         )
 
-    def pos_copy(step, j, base_id):
-        part = pl.ds(step * 8 + j, 1)
-        return pltpu.make_async_remote_copy(
-            src_ref=send_pos.at[part], dst_ref=recv_pos.at[part],
-            send_sem=pos_send_sem, recv_sem=pos_recv_sem,
-            device_id=(base_id + columns[j],), device_id_type=MESH,
-        )
-
-    pl.semaphore_wait(barrier, NDEV)
-    here = plane(0)
-    for j in range(1, 8):
-        pos_copy(0, j, here).start()
-        row_copy(0, j, here).start()
-
     def send(step, carry):
         base_id = plane(step)
         for j in range(8):
-            pos_copy(step, j, base_id).start()
             row_copy(step, j, base_id).start()
         return carry
 
-    lax.fori_loop(1, 16, send, 0)
-
-    recv_rows[:CAP, :] = send_rows[:CAP, :]
-    recv_pos[0:1, :] = send_pos[0:1, :]
-
-    rest = pl.ds(1, NDEV - 1)
+    pl.semaphore_wait(ready_sem, 7)
+    for j in range(1, 8):
+        row_copy(0, j, planes[0]).start()
+    lax.fori_loop(1, SPLIT, send, 0)
+
+    rest = pl.ds(1, 15)
     whole = pltpu.make_async_remote_copy(
-        src_ref=send_pos.at[rest], dst_ref=recv_pos.at[rest], send_sem=pos_send_sem, recv_sem=pos_recv_sem,
-        device_id=(me,), device_id_type=MESH,
+        src_ref=send_pos.at[rest], dst_ref=plane_pos.at[rest],
+        send_sem=plane_send_sem, recv_sem=plane_recv_sem, device_id=(me,), device_id_type=MESH,
     )
     whole.wait_send()
     whole.wait_recv()
-    keep = (iota((NDEV, 128), 0) % 8) == (iota((NDEV, 128), 1) // CAP)
-    wanted = jnp.sum(jnp.where(keep, recv_pos[...], 0.0).reshape(16, 8, 128), axis=1) - 1.0
+    for j in range(1, 8):
+        pltpu.make_async_remote_copy(
+            src_ref=plane_pos, dst_ref=recv_pos.at[pl.ds(j * 16, 16)],
+            send_sem=pos_send_sem, recv_sem=pos_recv_sem,
+            device_id=(column_mates[j - 1],), device_id_type=MESH,
+        ).start()
+    lax.fori_loop(SPLIT, 16, send, 0)
+
+    recv_rows[:CAP, :] = send_rows[:CAP, :]
+    recv_pos[0:16, :] = plane_pos[...]
+
+    rest = pl.ds(16, 112)
+    whole = pltpu.make_async_remote_copy(
+        src_ref=recv_pos.at[rest], dst_ref=recv_pos.at[rest],
+        send_sem=pos_send_sem, recv_sem=pos_recv_sem, device_id=(me,), device_id_type=MESH,
+    )
+    whole.wait_send()
+    whole.wait_recv()
+    sender = iota((16, 128), 1) // CAP
+    wanted = jnp.full((16, 128), -1.0, F32)
+    for j in range(8):
+        wanted = wanted + jnp.where(sender == j, recv_pos[j * 16 : (j + 1) * 16, :], 0.0)
 
     for group in range(GROUPS):
         first = CAP if group == 0 else group * GROUP_ROWS
@@ -191,7 +218,8 @@
         device_id=(before,), device_id_type=MESH,
     )
 
-    load_weight.wait()
+    for load in loads[2:]:
+        load.wait()
     weight = weight_ref[...]
     bias = bias_ref[...]
     score_weight = score_ref[...].astype(F32)
@@ -235,20 +263,27 @@
     return pl.pallas_call(
         kernel,
         out_shape=jax.ShapeDtypeStruct((WIN - 1, ROWS), F32),
-        in_specs=[vmem, hbm, hbm, vmem, vmem],
+        in_specs=[hbm] * 5,
         out_specs=vmem,
         scratch_shapes=[
+            pltpu.VMEM((8, 128), jnp.int32),
             pltpu.VMEM((ROWS, 128), BF16),
             pltpu.VMEM((256, 128), BF16),
+            pltpu.VMEM((1, 128), F32),
+            pltpu.VMEM((1, 128), BF16),
             pltpu.VMEM((NDEV * CAP, 128), BF16),
             pltpu.VMEM((NDEV * CAP, 128), BF16),
-            pltpu.VMEM((NDEV, 128), F32),
+            pltpu.VMEM((16, 128), F32),
+            pltpu.VMEM((16, 128), F32),
             pltpu.VMEM((NDEV, 128), F32),
             pltpu.VMEM((ROWS + WIN * UNITS, 128), F32),
             pltpu.VMEM((WIN, 128), BF16),
             pltpu.VMEM((WIN, 128), BF16),
             pltpu.VMEM((ROWS, 128), F32),
-            pltpu.SemaphoreType.DMA((2,)),
+            pltpu.SemaphoreType.DMA((5,)),
+            pltpu.SemaphoreType.REGULAR,
+            pltpu.SemaphoreType.DMA,
+            pltpu.SemaphoreType.DMA,
             pltpu.SemaphoreType.DMA,
             pltpu.SemaphoreType.DMA,
             pltpu.SemaphoreType.DMA,

time: 31.3 us -> 28.9 us (0.923)
  Pallas kernels: 29.6 us -> 27.2 us
    pallas_call x1, Pallas kernels: 29.6 us -> 27.2 us  [body(): pl.pallas_call(kernel, out_shape=jax.ShapeDtypeStruct((WIN - 1, ROWS), F3...]
where the time goes in v3:
time: 28.9 us; the launch traced here: 28.8 us
  Pallas kernels  27.2 us (94%)
  local copies, waits for them, and re-layouts  1.57 us (5%)
    pallas_call x1, Pallas kernels, body(): pl.pallas_call(kernel, out_shape=jax.ShapeDtypeStruct((WIN - 1, ROWS), F3...  27.2 us
    unnamed x1, local copies, waits for them, and re-layouts  1.57 us

profile of v3, /device:TPU:1, one launch (start us, length us, event | category | flops | bytes accessed | tf_op | source)
XLA Modules:
  0.0 28.8 jit_solution(5010320707932390797)
XLA Ops:
  0.0 27.2 %neighborhood_scores.1 = f32[31,1024]{1,0:T(8,128)} custom-call(s32[8,128]{1,0:T(8,128)} %bitcast.3, bf16[1024,128]{1,0:T(8,128)(2,1)} %emb_hbm.1, bf16[256,128]{1,0:T(8,128)(2,1)} %weight_hbm.1, f32[1,128]{1,0:T(1,128)} %bitcast.4, bf16[1,128]{1,0:T(2,128)(2,1)} %bitcast.5), custom_call_target="tpu_custom_call" | custom-call | tf_op jit(solution)/shard_map/neighborhood_scores/pallas_call | solution.py:263
  27.2 1.6 %copy.7 = f32[31,1024]{1,0:T(8,128)} copy(f32[31,1024]{1,0:T(8,128)} %neighborhood_scores.1) | data formatting | bytes 253952

commit v4 on v3

--- a/solution.py
+++ b/solution.py
@@ -19,7 +19,16 @@
 GROUP_ROWS = GROUP_DEVS * CAP
 CHUNK = 512
 PLACES = 256
-SPLIT = 7
+SPLIT = 12
+SELF = NDEV - 1
+
+
+def hops(steps):
+    return min(steps, 4 - steps)
+
+
+PLANES = sorted(range(16), key=lambda q: -hops(q // 4) - hops(q % 4))
+COLUMNS = sorted(range(8), key=lambda q: -2 * hops(q // 2) - q % 2)
 F32, BF16 = jnp.float32, jnp.bfloat16
 
 
@@ -31,6 +40,10 @@
     lanes = jnp.broadcast_to(labels, (rows, 128)).astype(BF16)
     numbers = iota((rows, 128), 0).astype(F32).astype(BF16)
     return jnp.where(numbers == lanes, jnp.ones((), BF16), jnp.zeros((), BF16))
+
+
+def lookup(values, order):
+    return sum(jnp.where(values == q, jnp.int32(i), jnp.int32(0)) for i, q in enumerate(order) if i)
 
 
 def within(values, low, size):
@@ -60,16 +73,12 @@
     for load in loads:
         load.start()
 
-    columns = [((my_y + dy) % 4) * 2 + (my_c + dc) % 2 for dy in range(4) for dc in range(2)]
-
-    def plane(step):
-        step = (step * 5) % 16
-        return (((my_z + step // 4) % 4) * 4 + (my_x + step % 4) % 4) * 8
+    planes = [((my_z + q // 4) % 4) * 32 + ((my_x + q % 4) % 4) * 8 for q in PLANES]
+    columns = [((my_y + q // 2) % 4) * 2 + (my_c + q % 2) % 2 for q in COLUMNS]
 
     barrier = pltpu.get_barrier_semaphore()
-    planes = [plane(step) for step in range(16)]
-    plane_mates = [planes[step] + columns[0] for step in range(1, 16)]
-    column_mates = [planes[0] + columns[j] for j in range(1, 8)]
+    plane_mates = [planes[step] + columns[7] for step in range(15)]
+    column_mates = [planes[15] + columns[j] for j in range(7)]
     for mate in plane_mates + column_mates:
         pl.semaphore_signal(barrier, inc=1, device_id=(mate,), device_id_type=MESH)
 
@@ -79,7 +88,7 @@
     local = ranks - owner * ROWS
     plane_rel = ((owner // 32 - my_z) & 3) * 4 + ((owner // 8 - my_x) & 3)
     column_rel = ((owner // 2 - my_y) & 3) * 2 + ((owner - my_c) & 1)
-    rel = ((plane_rel * 13) & 15) * 8 + column_rel
+    rel = lookup(plane_rel, PLANES) * 8 + lookup(column_rel, COLUMNS)
     place = (local % STRIDE) * UNITS + local // STRIDE + 1
     rel_f = rel.astype(F32)
     place_high = (place // 32).astype(F32)
@@ -122,17 +131,7 @@
     keep = (iota((NDEV, 128), 0) % 8) == (iota((NDEV, 128), 1) // CAP)
     by_step = jnp.sum(jnp.where(keep, places, 0.0).reshape(16, 8, 128), axis=1)
     send_pos[...] = by_step
-    plane_pos[0:1, :] = by_step[0:1]
-
-    pl.semaphore_wait(barrier, 22)
-    for mate in column_mates:
-        pl.semaphore_signal(ready_sem, inc=1, device_id=(mate,), device_id_type=MESH)
-    for step in range(1, 16):
-        pltpu.make_async_remote_copy(
-            src_ref=send_pos.at[pl.ds(step, 1)], dst_ref=plane_pos.at[pl.ds(step, 1)],
-            send_sem=plane_send_sem, recv_sem=plane_recv_sem,
-            device_id=(plane_mates[step - 1],), device_id_type=MESH,
-        ).start()
+    plane_pos[15:16, :] = by_step[15:16]
 
     target = rel_f * CAP + slot
 
@@ -144,44 +143,54 @@
         rows = jnp.dot(choose, emb, preferred_element_type=F32).astype(BF16)
         send_rows[group * GROUP_ROWS : (group + 1) * GROUP_ROWS, :] = rows
 
-    def row_copy(step, j, base_id):
-        part = pl.ds(pl.multiple_of((step * 8 + j) * CAP, CAP), CAP)
-        return pltpu.make_async_remote_copy(
+    recv_rows[SELF * CAP :, :] = send_rows[SELF * CAP :, :]
+
+    def send(step, j):
+        part = pl.ds((step * 8 + j) * CAP, CAP)
+        pltpu.make_async_remote_copy(
             src_ref=send_rows.at[part], dst_ref=recv_rows.at[part],
             send_sem=send_sem, recv_sem=recv_sems.at[step // 2],
-            device_id=(base_id + columns[j],), device_id_type=MESH,
-        )
-
-    def send(step, carry):
-        base_id = plane(step)
-        for j in range(8):
-            row_copy(step, j, base_id).start()
-        return carry
-
+            device_id=(planes[step] + columns[j],), device_id_type=MESH,
+        ).start()
+
+    pl.semaphore_wait(barrier, 22)
+    for mate in column_mates:
+        pl.semaphore_signal(ready_sem, inc=1, device_id=(mate,), device_id_type=MESH)
+    for step in range(15):
+        send(step, 7)
+    for j in range(7):
+        send(15, j)
+    for step in range(15):
+        pltpu.make_async_remote_copy(
+            src_ref=send_pos.at[pl.ds(step, 1)], dst_ref=plane_pos.at[pl.ds(step, 1)],
+            send_sem=plane_send_sem, recv_sem=plane_recv_sem,
+            device_id=(plane_mates[step],), device_id_type=MESH,
+        ).start()
     pl.semaphore_wait(ready_sem, 7)
-    for j in range(1, 8):
-        row_copy(0, j, planes[0]).start()
-    lax.fori_loop(1, SPLIT, send, 0)
-
-    rest = pl.ds(1, 15)
+    for step in range(SPLIT):
+        for j in range(7):
+            send(step, j)
+
+    rest = pl.ds(0, 15)
     whole = pltpu.make_async_remote_copy(
         src_ref=send_pos.at[rest], dst_ref=plane_pos.at[rest],
         send_sem=plane_send_sem, recv_sem=plane_recv_sem, device_id=(me,), device_id_type=MESH,
     )
     whole.wait_send()
     whole.wait_recv()
-    for j in range(1, 8):
+    for j in range(7):
         pltpu.make_async_remote_copy(
             src_ref=plane_pos, dst_ref=recv_pos.at[pl.ds(j * 16, 16)],
             send_sem=pos_send_sem, recv_sem=pos_recv_sem,
-            device_id=(column_mates[j - 1],), device_id_type=MESH,
+            device_id=(column_mates[j],), device_id_type=MESH,
         ).start()
-    lax.fori_loop(SPLIT, 16, send, 0)
-
-    recv_rows[:CAP, :] = send_rows[:CAP, :]
-    recv_pos[0:16, :] = plane_pos[...]
-
-    rest = pl.ds(16, 112)
+    for step in range(SPLIT, 15):
+        for j in range(7):
+            send(step, j)
+
+    recv_pos[112:, :] = plane_pos[...]
+
+    rest = pl.ds(0, 112)
     whole = pltpu.make_async_remote_copy(
         src_ref=recv_pos.at[rest], dst_ref=recv_pos.at[rest],
         send_sem=pos_send_sem, recv_sem=pos_recv_sem, device_id=(me,), device_id_type=MESH,
@@ -193,20 +202,22 @@
     for j in range(8):
         wanted = wanted + jnp.where(sender == j, recv_pos[j * 16 : (j + 1) * 16, :], 0.0)
 
-    for group in range(GROUPS):
-        first = CAP if group == 0 else group * GROUP_ROWS
-        part = pl.ds(first, (group + 1) * GROUP_ROWS - first)
-        pltpu.make_async_remote_copy(
-            src_ref=send_rows.at[part], dst_ref=recv_rows.at[part],
-            send_sem=send_sem, recv_sem=recv_sems.at[group], device_id=(me,), device_id_type=MESH,
-        ).wait_recv()
-        got = recv_rows[group * GROUP_ROWS : (group + 1) * GROUP_ROWS, :]
+    per = GROUPS // 4
+    for part in range(4):
+        for group in range(part * per, (part + 1) * per):
+            first = group * GROUP_ROWS
+            arriving = pl.ds(first, min(first + GROUP_ROWS, SELF * CAP) - first)
+            pltpu.make_async_remote_copy(
+                src_ref=send_rows.at[arriving], dst_ref=recv_rows.at[arriving],
+                send_sem=send_sem, recv_sem=recv_sems.at[group], device_id=(me,), device_id_type=MESH,
+            ).wait_recv()
+        got = recv_rows[part * per * GROUP_ROWS : (part + 1) * per * GROUP_ROWS, :]
         for block in range(ROWS // PLACES):
-            labels = within(wanted[2 * group : 2 * group + 2], float(block * PLACES), PLACES)
-            choose = jnp.concatenate([one_hot(labels[i : i + 1], PLACES) for i in range(2)], axis=1)
+            labels = within(wanted[2 * part * per : 2 * (part + 1) * per], float(block * PLACES), PLACES)
+            choose = jnp.concatenate([one_hot(labels[i : i + 1], PLACES) for i in range(2 * per)], axis=1)
             rows = jnp.dot(choose, got, preferred_element_type=F32)
             where = slice(block * PLACES, (block + 1) * PLACES)
-            if group == 0:
+            if part == 0:
                 tiles[where, :] = rows
             else:
                 tiles[where, :] = tiles[where, :] + rows
@@ -250,7 +261,7 @@
         inside = position + block * 128 + offset < NDEV * ROWS
         out_ref[:, block * 128 : (block + 1) * 128] = jnp.where(inside, turned, 0.0)[: WIN - 1]
 
-    part = pl.ds(CAP, (NDEV - 1) * CAP)
+    part = pl.ds(0, SELF * CAP)
     pltpu.make_async_remote_copy(
         src_ref=send_rows.at[part], dst_ref=recv_rows.at[part],
         send_sem=send_sem, recv_sem=recv_sems.at[0], device_id=(me,), device_id_type=MESH,
@@ -262,7 +273,7 @@
     hbm = pl.BlockSpec(memory_space=pl.ANY)
     return pl.pallas_call(
         kernel,
-        out_shape=jax.ShapeDtypeStruct((WIN - 1, ROWS), F32),
+        out_shape=pltpu.VMEM((WIN - 1, ROWS), F32),
         in_specs=[hbm] * 5,
         out_specs=vmem,
         scratch_shapes=[

time: 28.9 us -> 26.5 us (0.917)
  Pallas kernels: 27.2 us -> 25.7 us
  local copies, waits for them, and re-layouts: 1.57 us -> 0.66 us
    pallas_call x1, Pallas kernels: 27.2 us -> 25.7 us  [body(): pl.pallas_call(kernel, out_shape=pltpu.VMEM((WIN - 1, ROWS), F32), in_spe...]
    unnamed x1, local copies, waits for them, and re-layouts: 1.57 us -> 0.66 us
where the time goes in v4:
time: 26.5 us; the launch traced here: 26.4 us
  Pallas kernels  25.7 us (97%)
  local copies, waits for them, and re-layouts  0.66 us (2%)
    pallas_call x1, Pallas kernels, body(): pl.pallas_call(kernel, out_shape=pltpu.VMEM((WIN - 1, ROWS), F32), in_spe...  25.7 us
    unnamed x1, local copies, waits for them, and re-layouts  0.66 us

profile of v4, /device:TPU:1, one launch (start us, length us, event | category | flops | bytes accessed | tf_op | source)
XLA Modules:
  0.0 26.4 jit_solution(8773380655559234302)
XLA Ops:
  0.0 25.7 %neighborhood_scores.1 = f32[31,1024]{1,0:T(8,128)S(1)} custom-call(s32[8,128]{1,0:T(8,128)} %bitcast.3, bf16[1024,128]{1,0:T(8,128)(2,1)} %emb_hbm.1, bf16[256,128]{1,0:T(8,128)(2,1)} %weight_hbm.1, f32[1,128]{1,0:T(1,128)} %bitcast.4, bf16[1,128]{1,0:T(2,128)(2,1)} %bitcast.5), custom_call_target="tpu_custom_call" | custom-call | tf_op jit(solution)/shard_map/neighborhood_scores/pallas_call | solution.py:274
  25.8 0.7 %copy.7 = f32[31,1024]{1,0:T(8,128)} copy(f32[31,1024]{1,0:T(8,128)S(1)} %neighborhood_scores.1) | data formatting | bytes 253952

commit v5 on v4

--- a/solution.py
+++ b/solution.py
@@ -287,10 +287,10 @@
             pltpu.VMEM((16, 128), F32),
             pltpu.VMEM((16, 128), F32),
             pltpu.VMEM((NDEV, 128), F32),
-            pltpu.VMEM((ROWS + WIN * UNITS, 128), F32),
+            pltpu.VMEM((ROWS + (WIN + 1) * UNITS, 128), F32),
             pltpu.VMEM((WIN, 128), BF16),
             pltpu.VMEM((WIN, 128), BF16),
-            pltpu.VMEM((ROWS, 128), F32),
+            pltpu.VMEM((ROWS + UNITS, 128), F32),
             pltpu.SemaphoreType.DMA((5,)),
             pltpu.SemaphoreType.REGULAR,
             pltpu.SemaphoreType.DMA,

time: 26.5 us -> 26.5 us (level)
  no operation moved by 1% of the time
where the time goes in v5:
time: 26.5 us; the launch traced here: 26.4 us
  Pallas kernels  25.7 us (97%)
  local copies, waits for them, and re-layouts  0.66 us (2%)
    pallas_call x1, Pallas kernels, body(): pl.pallas_call(kernel, out_shape=pltpu.VMEM((WIN - 1, ROWS), F32), in_spe...  25.7 us
    unnamed x1, local copies, waits for them, and re-layouts  0.66 us

profile of v5, /device:TPU:1, one launch (start us, length us, event | category | flops | bytes accessed | tf_op | source)
XLA Modules:
  0.0 26.4 jit_solution(11458286741708610069)
XLA Ops:
  0.0 25.7 %neighborhood_scores.1 = f32[31,1024]{1,0:T(8,128)S(1)} custom-call(s32[8,128]{1,0:T(8,128)} %bitcast.3, bf16[1024,128]{1,0:T(8,128)(2,1)} %emb_hbm.1, bf16[256,128]{1,0:T(8,128)(2,1)} %weight_hbm.1, f32[1,128]{1,0:T(1,128)} %bitcast.4, bf16[1,128]{1,0:T(2,128)(2,1)} %bitcast.5), custom_call_target="tpu_custom_call" | custom-call | tf_op jit(solution)/shard_map/neighborhood_scores/pallas_call | solution.py:274
  25.8 0.7 %copy.7 = f32[31,1024]{1,0:T(8,128)} copy(f32[31,1024]{1,0:T(8,128)S(1)} %neighborhood_scores.1) | data formatting | bytes 253952
